TPU v7x, 32 devices: a whole 2x2x4 slice. The times are simulated.
32 devices in a mesh: groups: 2 (over y), range: 8 (over z, x), sub: 2 (over core).
Axes of the slice: x: 2, y: 2, z: 4, core: 2. Of those that a mesh axis runs over, the one named last changes fastest.
Arguments:
- samples: float32 [2, 1024, 32, 128], P(None, ('groups', 'range', 'sub')), parts along dimension 1, may hold values from -6 to 6
- beam_weights: float32 [32, 8, 2, 64, 128], P(('groups', 'range'), None, None, None, 'sub'), parts along dimension 0, may hold values from -0.25 to 0.25
- subarrays: int32 [32, 8, 64], P(('groups', 'range', 'sub')), parts along dimension 0, may hold values from 0 to 511, as said below
- training: int32 [64], P(('groups', 'range', 'sub')), parts along dimension 0, may hold values 0 or 1
Outputs:
- covariance: float32 [32, 8, 64, 128], P(('groups', 'range', 'sub')), parts along dimension 0
- filtered: float32 [2, 128, 64, 128], P(None, None, ('groups', 'range', 'sub')), parts along dimension 2
- energy: float32 [256], P('groups'), parts along dimension 0
There are 2 independent parts, one for each index of `groups`. A program takes and returns all parts, laid end to end along the dimension named above; each array names one. Nothing has to cross between parts.
Inputs may be any that keep to these rules, and one draw needn't show every extreme that they name: `subarrays`: in each gate block the 512 indices are all 512 channels, each once.
All inputs are finite; a program needn't handle non-finite values. No bound on the sum of `training` on one device may be relied on, other than what follows from the above.
Results may differ from a plain program's by a relative error of at most 0.0003.
Values sent between devices are 32-bit elements; how exact they have to be, the bound alone decides.
A program may use at most 64 MiB of HBM per device.

v0:
```python
import jax
import jax.numpy as jnp
from jax import lax
from jax.sharding import PartitionSpec as P

GB = 2


loading = 0.05


def block_terms(snaps, chosen, weights, masked, factor):
    highest = lax.Precision.HIGHEST
    picked = jnp.take(snaps, chosen, axis=1)
    real_part = picked[0]
    imag_part = picked[1]
    real_masked = real_part * masked
    imag_masked = imag_part * masked
    cov_real = (
        jnp.einsum("snx,smx->snm", real_masked, real_part, precision=highest)
        + jnp.einsum("snx,smx->snm", imag_masked, imag_part, precision=highest)
    ) * factor
    cov_imag = (
        jnp.einsum("snx,smx->snm", imag_masked, real_part, precision=highest)
        - jnp.einsum("snx,smx->snm", real_masked, imag_part, precision=highest)
    ) * factor
    w_real = weights[:, 0]
    w_imag = weights[:, 1]
    out_real = jnp.einsum("snk,snx->kx", w_real, real_part, precision=highest) + jnp.einsum(
        "snk,snx->kx", w_imag, imag_part, precision=highest
    )
    out_imag = jnp.einsum("snk,snx->kx", w_real, imag_part, precision=highest) - jnp.einsum(
        "snk,snx->kx", w_imag, real_part, precision=highest
    )
    prod_real = jnp.einsum("snm,smk->snk", cov_real, w_real, precision=highest) - jnp.einsum(
        "snm,smk->snk", cov_imag, w_imag, precision=highest
    )
    prod_imag = jnp.einsum("snm,smk->snk", cov_real, w_imag, precision=highest) + jnp.einsum(
        "snm,smk->snk", cov_imag, w_real, precision=highest
    )
    quadratic = jnp.sum(w_real * prod_real + w_imag * prod_imag, axis=(0, 1))
    inverse = 1.0 / jnp.sqrt(quadratic + loading)
    filtered = jnp.stack([out_real * inverse[:, None], out_imag * inverse[:, None]])
    energy = jnp.sum(out_real * out_real + out_imag * out_imag, axis=1)
    covariance = jnp.concatenate([cov_real, cov_imag], axis=-1)
    return (covariance, filtered, energy)


def body(samples, beam_weights, subarrays, training):
    range_count = lax.axis_size("range")
    core_count = lax.axis_size("sub")
    parts_iq, chan_dev, all_gates, pulses = samples.shape
    gate_dev = all_gates // (range_count * core_count)
    channels = chan_dev * range_count * core_count
    blocks_dev = gate_dev // GB
    spread = samples.reshape(parts_iq, 1, 1, chan_dev, range_count, core_count, gate_dev, pulses)
    turned = lax.all_to_all(
        lax.all_to_all(spread, "range", split_axis=4, concat_axis=1, tiled=True),
        "sub",
        split_axis=5,
        concat_axis=2,
        tiled=True,
    )
    local_data = turned.reshape(parts_iq, channels, blocks_dev, GB * pulses).transpose(2, 0, 1, 3)
    mine = lax.all_to_all(beam_weights, "sub", split_axis=0, concat_axis=4, tiled=True)
    gates_on = training.astype(jnp.float32).reshape(blocks_dev, GB)
    masked = jnp.repeat(gates_on, pulses, axis=1)
    factor = 1.0 / (GB * pulses)
    covs, filts, energies = jax.vmap(block_terms, in_axes=(0, 0, 0, 0, None))(
        local_data, subarrays, mine, masked, factor
    )
    beams = filts.shape[2]
    filtered = filts.reshape(blocks_dev, parts_iq, beams, GB, pulses).transpose(1, 2, 0, 3, 4)
    filtered = filtered.reshape(parts_iq, beams, gate_dev, pulses)
    total = lax.psum(jnp.sum(energies, axis=0), ("range", "sub"))
    energy = total / (all_gates * pulses)
    return (covs, filtered, energy)


def solution(mesh):
    placed = (
        P(None, ("groups", "range", "sub"), None, None),
        P(("groups", "range"), None, None, None, "sub"),
        P(("groups", "range", "sub"), None, None),
        P(("groups", "range", "sub")),
    )
    return jax.shard_map(
        body,
        mesh=mesh,
        in_specs=placed,
        out_specs=(
            P(("groups", "range", "sub"), None, None, None),
            P(None, None, ("groups", "range", "sub"), None),
            P("groups"),
        ),
        check_vma=False,
    )
```

profile of v0, /device:TPU:0, one launch (start us, length us, event | category | flops | bytes accessed | tf_op | source)
XLA Modules:
  0.0 92.5 jit_solution(9004139148378862796)
XLA Ops:
  0.6 0.0 copy-start
  0.6 2.5 %reshape.157 = f32[2,1,65536]{2,1,0:T(1,128)} reshape(f32[2,8,2,64,64]{4,3,2,1,0:T(8,128)} %param.5) | data formatting | bytes 1048576
  3.2 3.5 %all-to-all-start.2 = ((f32[2,1,65536]{2,1,0:T(1,128)}), f32[2,1,65536]{2,1,0:T(1,128)S(1)}, u32[]{:S(2)}, u32[]{:S(2)}) async-start(f32[2,1,65536]{2,1,0:T(1,128)} %reshape.157), calls=%async_computation.2 | async-start | bytes 1048576 | tf_op jit(solution)/shard_map/all_to_all | solution.py:65
  6.6 0.0 copy-done
  6.7 1.6 %copy.24 = f32[2,1,1,32,8,2,2,128]{7,6,3,5,0,2,1,4:T(2,128)} copy(f32[2,1,1,32,8,2,2,128]{7,6,5,4,3,0,2,1:T(2,128)S(1)} %bitcast.103) | data formatting | bytes 2097152 | tf_op jit(solution)/shard_map/reshape | solution.py:56
  8.2 0.0 copy-start.2
  8.2 0.2 all-to-all-done.2
  8.4 0.0 copy-start.1
  8.4 7.4 %all-to-all-start = ((f32[2,1,1,32,8,2,2,128]{7,6,3,5,0,2,1,4:T(2,128)}), f32[2,1,1,32,8,2,2,128]{7,6,3,5,0,2,1,4:T(2,128)S(1)}, u32[]{:S(2)}, u32[]{:S(2)}) async-start(f32[2,1,1,32,8,2,2,128]{7,6,3,5,0,2,1,4:T(2,128)} %copy.24), calls=%async_computation | async-start | bytes 2097152 | tf_op jit(solution)/shard_map/all_to_all | solution.py:58
  15.8 0.0 copy-done.2
  15.8 0.0 copy-done.1
  15.9 0.1 reshape.147
  15.9 0.5 broadcast.75
  16.4 2.3 %reduce.5 = f32[2,65536]{1,0:T(2,128)S(1)} reduce(f32[2,1,65536]{2,1,0:T(1,128)S(1)} %all-to-all-done.2, f32[]{:T(128)} %broadcast.75), dimensions={1}, to_apply=%all_to_all.44.reduce_sub_computation | reduce | bytes 1048580 | tf_op jit(solution)/shard_map/all_to_all | solution.py:65
  18.8 0.6 reshape.158
  19.4 1.9 %copy.29 = f32[1,8,2,64,2,64]{5,4,3,1,2,0:T(2,128)} copy(f32[1,8,2,64,2,64]{5,3,2,1,4,0:T(8,128)S(1)} %bitcast.98) | data formatting | bytes 1048576 | tf_op jit(solution)/shard_map/all_to_all | solution.py:65
  21.2 1.8 %all_to_all.47 = f32[1,8,2,64,128]{4,3,1,2,0:T(8,128)S(1)} reshape(f32[1,8,2,64,2,64]{5,4,3,1,2,0:T(2,128)} %copy.29) | data formatting | bytes 1048576 | tf_op jit(solution)/shard_map/all_to_all | solution.py:65
  23.1 0.1 broadcast_bitcast_fusion
  23.1 18.9 %all-to-all-done = f32[2,1,1,32,8,2,2,128]{7,6,3,5,0,2,1,4:T(2,128)S(1)} async-done(((f32[2,1,1,32,8,2,2,128]{7,6,3,5,0,2,1,4:T(2,128)}), f32[2,1,1,32,8,2,2,128]{7,6,3,5,0,2,1,4:T(2,128)S(1)}, u32[]{:S(2)}, u32[]{:S(2)}) %all-to-all-start) | async-done | bytes 1048608 | tf_op jit(solution)/shard_map/all_to_all | solution.py:58
  42.1 0.1 copy.25
  42.1 4.6 %all_to_all.51 = f32[2,8,1,32,1,2,2,128]{7,6,3,1,0,4,2,5:T(2,128)S(1)} all-to-all(f32[2,8,1,32,1,2,2,128]{7,6,3,1,0,4,2,5:T(2,128)S(1)} %copy.25), channel_id=1, replica_groups=mesh['groups'=2,'range'=8,'sub'=2] {'sub'}, dimensions={5} | all-to-all | bytes 2097152 | tf_op jit(solution)/shard_map/all_to_all | solution.py:57
  46.7 0.1 copy.26
  46.8 0.8 copy.27
  47.6 2.3 %gather_fusion = f32[512,2,256]{2,1,0:T(2,128)S(1)} fusion(f32[1,2,512,256]{3,1,2,0:T(2,128)S(1)} %copy.27, s32[512]{0:T(512)S(1)} %reshape.147), kind=kCustom, calls=%fused_computation | custom fusion | bytes 2101248 | tf_op jit(solution)/shard_map/vmap(jit(_take))/gather | solution.py:14
  50.0 0.1 copy.28
  50.1 0.1 broadcast_select_fusion
  50.2 1.0 %convolution_bitcast_fusion.2 = f32[256,128]{1,0:T(8,128)S(1)} fusion(f32[1,2,8,64,256]{4,3,2,1,0:T(8,128)S(1)} %broadcast_select_fusion, f32[1,8,2,64,128]{4,3,1,2,0:T(8,128)S(1)} %all_to_all.47), kind=kOutput, calls=%fused_computation.13 | convolution fusion | flops 201326592 | bytes 917504 | tf_op jit(solution)/shard_map/vmap(snk,snx->kx)/dot_general | solution.py:29
  51.2 1.0 %convolution_bitcast_fusion = f32[256,128]{1,0:T(8,128)S(1)} fusion(f32[1,2,8,64,256]{4,3,2,1,0:T(8,128)S(1)} %broadcast_select_fusion, f32[1,8,2,64,128]{4,3,1,2,0:T(8,128)S(1)} %all_to_all.47), kind=kOutput, calls=%fused_computation.11 | convolution fusion | flops 201326592 | bytes 917504 | tf_op jit(solution)/shard_map/vmap(snk,snx->kx)/dot_general | solution.py:32
  52.2 0.6 fusion.12
  52.9 0.6 fusion.2
  53.5 0.4 fusion.19
  53.9 0.4 fusion.18
  54.3 0.6 fusion.8
  54.9 1.0 %fusion.6 = f32[256,128]{1,0:T(8,128)S(1)} fusion(f32[256,128]{1,0:T(8,128)S(1)} %convolution_bitcast_fusion.2, f32[1,2,8,64,256]{4,3,2,1,0:T(8,128)S(1)} %broadcast_select_fusion, f32[1,8,2,64,128]{4,3,1,2,0:T(8,128)S(1)} %all_to_all.47), kind=kOutput, calls=%fused_computation.15 | convolution fusion | flops 201359360 | bytes 1048576 | tf_op jit(solution)/shard_map/vmap(snk,snx->kx)/dot_general | solution.py:29
  55.9 0.6 fusion.3
  56.5 0.4 fusion
  56.9 0.4 fusion.5
  57.4 1.0 %add_reduce_fusion = (f32[128]{0:T(128)S(1)}, f32[256,128]{1,0:T(8,128)S(1)}, f32[256,128]{1,0:T(8,128)S(1)}) fusion(f32[256,128]{1,0:T(8,128)S(1)} %fusion.6, f32[128]{0:T(128)S(1)} %add_rsqrt_fusion, f32[256,128]{1,0:T(8,128)S(1)} %convolution_bitcast_fusion, f32[1,8,2,64,128]{4,3,1,2,0:T(8,128)S(1)} %all_to_all.47, ...), kind=kOutput, calls=%fused_computation.36 | convolution fusion | flops 201555840 | bytes 1311744 | tf_op jit(solution)/shard_map/vmap(snk,snx->kx)/dot_general | solution.py:32
  58.4 31.6 %psum.7 = f32[128]{0:T(128)S(1)} all-reduce(f32[128]{0:T(128)S(1)} %get-tuple-element.3), channel_id=1, replica_groups=mesh['groups'=2,'range'=8,'sub'=2] {'range','sub'}, use_global_device_ids=true, to_apply=%region_2.3 | all-reduce | flops 128 | bytes 1024 | tf_op jit(solution)/shard_map/psum | solution.py:75
  90.1 0.5 broadcast_multiply_fusion.2
  90.6 0.1 copy.30
  90.7 0.1 copy.31
  90.8 0.8 pad_maximum_fusion
  91.7 0.8 pad_maximum_fusion.1
  (6 shorter events, 0.0 us)
Async XLA Ops:
  0.6 6.0 %copy-start = (f32[2,32,32,128]{3,2,1,0:T(8,128)S(1)}, f32[2,32,32,128]{3,2,1,0:T(8,128)}, u32[]{:S(2)}) copy-start(f32[2,32,32,128]{3,2,1,0:T(8,128)} %param.4) | copy-start | bytes 3145732
  3.2 5.2 %all-to-all-start.2 = ((f32[2,1,65536]{2,1,0:T(1,128)}), f32[2,1,65536]{2,1,0:T(1,128)S(1)}, u32[]{:S(2)}, u32[]{:S(2)}) async-start(f32[2,1,65536]{2,1,0:T(1,128)} %reshape.157), calls=%async_computation.2 | async-start | bytes 1048576 | tf_op jit(solution)/shard_map/all_to_all | solution.py:65
  8.2 7.6 %copy-start.2 = (s32[2]{0:T(128)S(1)}, s32[2]{0:T(128)}, u32[]{:S(2)}) copy-start(s32[2]{0:T(128)} %param.7) | copy-start | bytes 28
  8.4 7.4 %copy-start.1 = (s32[1,8,64]{2,1,0:T(8,128)S(1)}, s32[1,8,64]{2,1,0:T(8,128)}, u32[]{:S(2)}) copy-start(s32[1,8,64]{2,1,0:T(8,128)} %param.6) | copy-start | bytes 6148
  8.4 33.7 %all-to-all-start = ((f32[2,1,1,32,8,2,2,128]{7,6,3,5,0,2,1,4:T(2,128)}), f32[2,1,1,32,8,2,2,128]{7,6,3,5,0,2,1,4:T(2,128)S(1)}, u32[]{:S(2)}, u32[]{:S(2)}) async-start(f32[2,1,1,32,8,2,2,128]{7,6,3,5,0,2,1,4:T(2,128)} %copy.24), calls=%async_computation | async-start | bytes 2097152 | tf_op jit(solution)/shard_map/all_to_all | solution.py:58
where the time goes:
time: 92.9 us; the launch traced here: 92.5 us
  blocking collectives  36.2 us (39%)
  waiting for transfers between devices  19.1 us (21%)
  local copies, waits for them, and re-layouts  12.7 us (14%)
  starting transfers between devices  10.9 us (12%)
  matrix products  8.12 us (9%)
  other arithmetic  4.67 us (5%)
    psum x1, blocking collectives, body(): total = lax.psum(jnp.sum(energies, axis=0), ('range', 'sub'))  31.6 us
    all_to_all x1, waiting for transfers between devices, body(): lax.all_to_all(spread, 'range', split_axis=4, concat_axis=1, tiled=True)  18.9 us
    all_to_all x1, starting transfers between devices, body(): lax.all_to_all(spread, 'range', split_axis=4, concat_axis=1, tiled=True)  7.41 us
    all_to_all x1, blocking collectives, body(): lax.all_to_all(lax.all_to_all(spread, 'range', split_axis=4, concat_axis=...  4.58 us
    all_to_all x3, local copies, waits for them, and re-layouts, body(): lax.all_to_all(beam_weights, 'sub', split_axis=0, concat_axis=4, tiled=True)  4.18 us
    all_to_all x1, starting transfers between devices, body(): lax.all_to_all(beam_weights, 'sub', split_axis=0, concat_axis=4, tiled=True)  3.49 us
    unnamed x8, local copies, waits for them, and re-layouts  3.15 us
    gather x4, local copies, waits for them, and re-layouts, block_terms(): picked = jnp.take(snaps, chosen, axis=1)  2.5 us
  transfers between devices with their start and end apart: 2, of which 2 were waited for; matrix products, arithmetic and copies ran while one was open for 8% of the time, Pallas kernels for 0%

commit v1 on v0

v1 whole, which is shorter than its diff:
```python
import functools

import jax
import jax.numpy as jnp
from jax import lax
from jax.experimental import pallas as pl
from jax.experimental.pallas import tpu as pltpu
from jax.sharding import PartitionSpec as P

GB = 2
loading = 0.05
F32 = jnp.float32
BF16 = jnp.bfloat16


def split(x):
    hi = x.astype(BF16)
    return hi, (x - hi.astype(F32)).astype(BF16)


def dot(a, b):
    return jnp.dot(a, b, preferred_element_type=F32)


def dot_t(a, b):
    return lax.dot_general(a, b, (((1,), (1,)), ((), ())), preferred_element_type=F32)


def partner(me, step, count):
    other, bit = me, 1
    while bit < count:
        other = other + ((step // bit) % 2) * (1 - 2 * ((me // bit) % 2)) * bit
        bit *= 2
    return other


def kernel(
    dims,
    smp, bw, sub, trn,
    cov, filt, en,
    stage, sendb, recv, wfull, lhs, wst, wq, sacc, gacc, esend, erecv,
    send_sem, recv_sem, wsem, esend_sem, erecv_sem, lsem,
):
    n, cores, c_loc, gates, pulses, ns, s_n, k_half = dims
    beams = 2 * k_half
    chans = n * c_loc
    half = n // 2
    rows = half * c_loc
    core = lax.axis_index("sub")
    me = lax.axis_index("range") * cores + core

    def where(d):
        return {"range": d // cores, "sub": d % cores}

    load = pltpu.make_async_copy(smp, stage, lsem.at[0])
    load.start()
    keep = pltpu.make_async_copy(bw.at[core], wfull.at[core], lsem.at[1])
    keep.start()

    barrier = pltpu.get_barrier_semaphore()

    def greet(t, c):
        pl.semaphore_signal(
            barrier, inc=1, device_id=where(partner(me, t, n)), device_id_type=pl.DeviceIdType.MESH
        )
        return c

    lax.fori_loop(1, n, greet, 0)
    load.wait()

    def arrange(d, c):
        for g in range(GB):
            sendb[d, g * 2 * c_loc : (g + 1) * 2 * c_loc, :] = stage[
                pl.ds(d * GB + g, 2 * c_loc, stride=gates), :
            ]
        return c

    lax.fori_loop(0, n, arrange, 0)
    recv[me] = sendb[me]
    pl.semaphore_wait(barrier, n - 1)

    def piece(d, slot, dev):
        return pltpu.make_async_remote_copy(
            src_ref=sendb.at[d],
            dst_ref=recv.at[slot],
            send_sem=send_sem.at[d],
            recv_sem=recv_sem.at[slot],
            device_id=where(dev),
            device_id_type=pl.DeviceIdType.MESH,
        )

    def launch(t, c):
        d = partner(me, t, n)
        piece(d, me, d).start()
        return c

    lax.fori_loop(1, n, launch, 0)
    swap = pltpu.make_async_remote_copy(
        src_ref=bw.at[1 - core],
        dst_ref=wfull.at[core],
        send_sem=wsem.at[0],
        recv_sem=wsem.at[1],
        device_id={"sub": 1 - core},
        device_id_type=pl.DeviceIdType.MESH,
    )
    swap.start()

    chosen = jnp.concatenate([sub[s : s + 1, :] for s in range(ns)], axis=1)
    keep.wait()
    swap.wait()
    sides = []
    for iq in range(2):
        cols = []
        for s in range(ns):
            cols.append(
                jnp.concatenate([jnp.transpose(wfull[h, s, iq]) for h in range(2)], axis=0)
            )
        sides.append(cols)
    for s in range(ns):
        w_r, w_i = sides[0][s], sides[1][s]
        top = jnp.concatenate([w_r, -w_i], axis=1)
        low = jnp.concatenate([w_i, w_r], axis=1)
        wq[s] = jnp.concatenate([top, low], axis=0)
        hi, lo = split(jnp.concatenate([w_r, w_i], axis=0))
        wst[s, 0] = hi
        wst[s, 1] = lo
    flat = jnp.concatenate([jnp.concatenate(cols, axis=1) for cols in sides], axis=0)
    w_hi, w_lo = split(flat)
    for ch in range(2):
        r = lax.broadcasted_iota(jnp.int32, (rows, chans), 0)
        if c_loc % 8 == 0:
            chan = r + ch * rows
        else:
            chan = (ch * half + r % half) * c_loc + r // half
        pick = jnp.where(chan == chosen, 1.0, 0.0).astype(F32)
        pick_b = pick.astype(BF16)
        lhs[ch, 0:chans, :] = jnp.transpose(pick).astype(BF16)
        lhs[ch, chans : chans + 2 * beams, :] = dot_t(w_hi, pick_b).astype(BF16)
        lhs[ch, chans + 2 * beams : chans + 4 * beams, :] = dot_t(w_lo, pick_b).astype(BF16)

    lanes = GB * pulses
    e_re = e_im = None
    for q in range(2):
        mine = me // half
        ch = mine if q == 0 else 1 - mine

        def arrive(t, c):
            src = partner(me, t, n)
            piece(src, src, src).wait_recv()
            return c

        lax.fori_loop(1 if q == 0 else half, half if q == 0 else n, arrive, 0)
        parts = []
        for iq in range(2):
            for g in range(GB):
                j = (g * 2 + iq) * c_loc
                if c_loc % 8 == 0:
                    block = recv[pl.ds(ch * half, half), j : j + c_loc, :].reshape(rows, pulses)
                else:
                    block = jnp.concatenate(
                        [
                            recv[pl.ds(ch * half, half), j + c : j + c + 1, :].reshape(half, pulses)
                            for c in range(c_loc)
                        ],
                        axis=0,
                    )
                parts.append(block)
        z = jnp.concatenate(parts, axis=1)
        z_hi, z_lo = split(z)
        l_hi = lhs[ch, chans : chans + 2 * beams, :]
        l_lo = lhs[ch, chans + 2 * beams : chans + 4 * beams, :]
        part = dot(l_hi, z_hi) + (dot(l_hi, z_lo) + dot(l_lo, z_hi))
        if q == 0:
            sacc[...] = part
        else:
            full = sacc[...] + part
            e_re = full[:beams, :lanes] + full[beams:, lanes:]
            e_im = full[:beams, lanes:] - full[beams:, :lanes]
            p_hi, p_lo = split(e_re * e_re + e_im * e_im)
            ones = jnp.ones((8, lanes), BF16)
            esum = dot_t(ones, p_hi) + dot_t(ones, p_lo)
            esend[...] = esum
            erecv[me] = esum

            def share(t, c):
                d = partner(me, t, n)
                report(d, me, d).start()
                return c

            def report(d, slot, dev):
                return pltpu.make_async_remote_copy(
                    src_ref=esend,
                    dst_ref=erecv.at[slot],
                    send_sem=esend_sem.at[d],
                    recv_sem=erecv_sem.at[slot],
                    device_id=where(dev),
                    device_id_type=pl.DeviceIdType.MESH,
                )

            lax.fori_loop(1, n, share, 0)
        sel = lhs[ch, 0:chans, :]
        g_hi, g_lo = dot(sel, z_hi), dot(sel, z_lo)
        if q == 0:
            gacc[0] = g_hi
            gacc[1] = g_lo
        else:
            gacc[0] = gacc[0] + g_hi
            gacc[1] = gacc[1] + g_lo

    factor = 1.0 / lanes
    lane = lax.broadcasted_iota(jnp.int32, (1, 2 * lanes), 1)
    first = trn[0].astype(F32)
    second = trn[1].astype(F32)
    gate = (lane // pulses) % GB
    mask = jnp.where(gate == 0, first, second)
    power = jnp.zeros((beams, 2 * s_n), F32)
    for s in range(ns):
        x = [gacc[i, s * s_n : (s + 1) * s_n, :] for i in range(2)]
        left = [(v * mask).astype(BF16) for v in x]
        right = [
            jnp.concatenate(
                [v, jnp.concatenate([-v[:, lanes:], v[:, :lanes]], axis=1)], axis=0
            ).astype(BF16)
            for v in x
        ]
        r_s = (
            dot_t(left[0], right[0]) + (dot_t(left[0], right[1]) + dot_t(left[1], right[0]))
        ) * factor
        cov[s] = r_s
        r_hi, r_lo = split(r_s)
        w_h, w_l = wst[s, 0], wst[s, 1]
        t_s = (dot(w_h, r_hi) + (dot(w_h, r_lo) + dot(w_l, r_hi))) * wq[s]
        power = power + t_s[:beams] + t_s[beams:]
    quadratic = jnp.sum(power, axis=1, keepdims=True)
    inverse = 1.0 / jnp.sqrt(quadratic + loading)
    for g in range(GB):
        filt[0, pl.ds(g, beams, stride=GB), :] = e_re[:, g * pulses : (g + 1) * pulses] * inverse
        filt[1, pl.ds(g, beams, stride=GB), :] = e_im[:, g * pulses : (g + 1) * pulses] * inverse

    def close(t, c):
        d = partner(me, t, n)
        report(d, d, d).wait_recv()
        report(d, d, d).wait_send()
        piece(d, d, d).wait_send()
        return c

    lax.fori_loop(1, n, close, 0)
    total = jnp.sum(erecv[...], axis=0)
    en[...] = total[0:1, :] * (1.0 / (gates * pulses))


def body(samples, beam_weights, subarrays, training):
    range_count = lax.axis_size("range")
    cores = lax.axis_size("sub")
    n = range_count * cores
    parts_iq, c_loc, gates, pulses = samples.shape
    blocks, ns, _, s_n, k_half = beam_weights.shape
    assert gates == GB * n and blocks == cores == 2 and subarrays.shape[0] == 1
    assert n & (n - 1) == 0
    assert parts_iq == 2 and n * c_loc == ns * s_n
    beams, chans, lanes = 2 * k_half, n * c_loc, GB * pulses
    dims = (n, cores, c_loc, gates, pulses, ns, s_n, k_half)
    hbm = pl.BlockSpec(memory_space=pl.ANY)
    vmem = pl.BlockSpec(memory_space=pltpu.VMEM)
    dma = pltpu.SemaphoreType.DMA
    cov, filt, en = pl.pallas_call(
        functools.partial(kernel, dims),
        out_shape=(
            jax.ShapeDtypeStruct((ns, s_n, 2 * s_n), F32),
            jax.ShapeDtypeStruct((2, beams * GB, pulses), F32),
            jax.ShapeDtypeStruct((1, beams), F32),
        ),
        in_specs=[hbm, hbm, vmem, pl.BlockSpec(memory_space=pltpu.SMEM)],
        out_specs=(vmem, vmem, vmem),
        scratch_shapes=[
            pltpu.VMEM((2 * c_loc * gates, pulses), F32),
            pltpu.VMEM((n, 2 * GB * c_loc, pulses), F32),
            pltpu.VMEM((n, 2 * GB * c_loc, pulses), F32),
            pltpu.VMEM((2, ns, 2, s_n, k_half), F32),
            pltpu.VMEM((2, chans + 4 * beams, chans // 2), BF16),
            pltpu.VMEM((ns, 2, 2 * beams, s_n), BF16),
            pltpu.VMEM((ns, 2 * beams, 2 * s_n), F32),
            pltpu.VMEM((2 * beams, 2 * lanes), F32),
            pltpu.VMEM((2, chans, 2 * lanes), F32),
            pltpu.VMEM((8, beams), F32),
            pltpu.VMEM((n, 8, beams), F32),
            dma((n,)),
            dma((n,)),
            dma((2,)),
            dma((n,)),
            dma((n,)),
            dma((2,)),
        ],
        compiler_params=pltpu.CompilerParams(collective_id=0, has_side_effects=True),
    )(
        samples.reshape(2 * c_loc * gates, pulses),
        beam_weights,
        subarrays.reshape(ns, s_n),
        training,
    )
    return (
        cov.reshape(1, ns, s_n, 2 * s_n),
        filt.reshape(2, beams, GB, pulses),
        en.reshape(beams),
    )


def solution(mesh):
    placed = (
        P(None, ("groups", "range", "sub"), None, None),
        P(("groups", "range"), None, None, None, "sub"),
        P(("groups", "range", "sub"), None, None),
        P(("groups", "range", "sub")),
    )
    return jax.shard_map(
        body,
        mesh=mesh,
        in_specs=placed,
        out_specs=(
            P(("groups", "range", "sub"), None, None, None),
            P(None, None, ("groups", "range", "sub"), None),
            P("groups"),
        ),
        check_vma=False,
    )
```

time: 92.9 us -> 41.9 us (0.45)
  Pallas kernels: 0 us -> 38.1 us
  blocking collectives: 36.2 us -> 0 us
  waiting for transfers between devices: 19.1 us -> 0 us
  starting transfers between devices: 10.9 us -> 0 us
  local copies, waits for them, and re-layouts: 12.7 us -> 2.94 us
  matrix products: 8.12 us -> 0 us
  other arithmetic: 4.67 us -> 0 us
    pallas_call x0 -> x1, Pallas kernels: none -> 38.1 us  [body(): pl.pallas_call(functools.partial(kernel, dims), out_shape=(jax.ShapeDtype...]
    psum x1 -> x0, blocking collectives: 31.6 us -> none  [body(): total = lax.psum(jnp.sum(energies, axis=0), ('range', 'sub'))]
    all_to_all x2 -> x0, waiting for transfers between devices: 19.1 us -> none  [the longest x1 18.9 us: body(): lax.all_to_all(spread, 'range', split_axis=4, concat_axis=1, tiled=True)]
    all_to_all x2 -> x0, starting transfers between devices: 10.9 us -> none  [the longest x1 7.41 us: body(): lax.all_to_all(spread, 'range', split_axis=4, concat_axis=1, tiled=True)]
    dot_general x12 -> x0, matrix products: 8.12 us -> none  [the longest x1 1.02 us: block_terms(): jnp.einsum('snk,snx->kx', w_real, imag_part, precision=highest)]
    all_to_all x1 -> x0, blocking collectives: 4.58 us -> none  [body(): lax.all_to_all(lax.all_to_all(spread, 'range', split_axis=4, concat_axis=...]
    all_to_all x5 -> x0, local copies, waits for them, and re-layouts: 4.35 us -> none  [the longest x3 4.18 us: body(): lax.all_to_all(beam_weights, 'sub', split_axis=0, concat_axis=4, tiled=True)]
    gather x4 -> x0, local copies, waits for them, and re-layouts: 2.5 us -> none  [block_terms(): picked = jnp.take(snaps, chosen, axis=1)]
  transfers between devices with their start and end apart: 2 -> 0, of which waited for: 2 -> 0; matrix products, arithmetic and copies ran while one was open for 8% -> 0% of each run, Pallas kernels for 0% -> 0%
where the time goes in v1:
time: 41.9 us; the launch traced here: 41.7 us
  Pallas kernels  38.1 us (91%)
  local copies, waits for them, and re-layouts  2.94 us (7%)
  between operations  0.65 us (2%)
    pallas_call x1, Pallas kernels, body(): pl.pallas_call(functools.partial(kernel, dims), out_shape=(jax.ShapeDtype...  38.1 us
    unnamed x7, local copies, waits for them, and re-layouts  2.94 us

profile of v1, /device:TPU:0, one launch (start us, length us, event | category | flops | bytes accessed | tf_op | source)
XLA Modules:
  0.0 41.7 jit_solution(1735749652694841729)
XLA Ops:
  0.6 38.1 %shard_map.67 = (f32[8,64,128]{2,1,0:T(8,128)}, f32[2,256,128]{2,1,0:T(8,128)}, f32[1,128]{1,0:T(1,128)}) custom-call(f32[2048,128]{1,0:T(8,128)} %bitcast.5, f32[2,8,2,64,64]{4,3,2,1,0:T(8,128)} %bw.1, s32[8,64]{1,0:T(8,128)} %bitcast.8, s32[2]{0:T(128)} %trn.1), custom_call_target="tpu_custom_call" | custom-call | tf_op jit(solution)/shard_map/pallas_call | solution.py:266
  38.8 0.0 copy-start
  38.8 1.7 %copy.10 = f32[1,8,64,128]{3,2,1,0:T(8,128)} copy(f32[1,8,64,128]{3,2,1,0:T(8,128)} %bitcast.7) | data formatting | bytes 524288
  40.5 0.0 copy-done
  40.5 0.0 copy-start.1
  40.5 0.7 %copy.11 = f32[2,128,2,128]{3,2,1,0:T(2,128)} copy(f32[2,128,2,128]{3,2,1,0:T(2,128)S(1)} %bitcast.6) | data formatting | bytes 524288
  41.2 0.0 copy-done.1
  41.2 0.5 %copy.12 = f32[128]{0:T(128)} copy(f32[128]{0:T(128)S(1)} %bitcast.9) | data formatting | bytes 1024
Async XLA Ops:
  38.8 1.7 %copy-start = (f32[2,256,128]{2,1,0:T(8,128)S(1)}, f32[2,256,128]{2,1,0:T(8,128)}, u32[]{:S(2)}) copy-start(f32[2,256,128]{2,1,0:T(8,128)} %get-tuple-element.7) | copy-start | bytes 786436
  40.5 0.7 %copy-start.1 = (f32[1,128]{1,0:T(1,128)S(1)}, f32[1,128]{1,0:T(1,128)}, u32[]{:S(2)}) copy-start(f32[1,128]{1,0:T(1,128)} %get-tuple-element.8) | copy-start | bytes 1540

commit v2 on v1

--- a/solution.py
+++ b/solution.py
@@ -36,36 +36,45 @@
 
 def kernel(
     dims,
-    smp, bw, sub, trn,
+    smp, bw, sub_in, trn_in,
     cov, filt, en,
-    stage, sendb, recv, wfull, lhs, wst, wq, sacc, gacc, esend, erecv,
+    sub, trn, stage, sendb, recv, wfull, lhs, wst, wq, sacc, gacc, esend, erecv,
     send_sem, recv_sem, wsem, esend_sem, erecv_sem, lsem,
 ):
     n, cores, c_loc, gates, pulses, ns, s_n, k_half = dims
     beams = 2 * k_half
     chans = n * c_loc
-    half = n // 2
-    rows = half * c_loc
+    part = n // 4
+    rows = part * c_loc
     core = lax.axis_index("sub")
     me = lax.axis_index("range") * cores + core
 
     def where(d):
         return {"range": d // cores, "sub": d % cores}
 
+    barrier = pltpu.get_barrier_semaphore()
+
+    def greet(t, c):
+        pl.semaphore_signal(
+            barrier,
+            inc=1,
+            device_id=where(partner(me, n - t, n)),
+            device_id_type=pl.DeviceIdType.MESH,
+        )
+        return c
+
+    lax.fori_loop(1, n, greet, 0)
     load = pltpu.make_async_copy(smp, stage, lsem.at[0])
     load.start()
     keep = pltpu.make_async_copy(bw.at[core], wfull.at[core], lsem.at[1])
     keep.start()
 
-    barrier = pltpu.get_barrier_semaphore()
-
-    def greet(t, c):
-        pl.semaphore_signal(
-            barrier, inc=1, device_id=where(partner(me, t, n)), device_id_type=pl.DeviceIdType.MESH
-        )
-        return c
-
-    lax.fori_loop(1, n, greet, 0)
+    small = [
+        pltpu.make_async_copy(sub_in, sub, lsem.at[2]),
+        pltpu.make_async_copy(trn_in, trn, lsem.at[3]),
+    ]
+    for copy in small:
+        copy.start()
     load.wait()
 
     def arrange(d, c):
@@ -94,7 +103,8 @@
         piece(d, me, d).start()
         return c
 
-    lax.fori_loop(1, n, launch, 0)
+    lax.fori_loop(n // 2, n, launch, 0)
+    lax.fori_loop(1, n // 2, launch, 0)
     swap = pltpu.make_async_remote_copy(
         src_ref=bw.at[1 - core],
         dst_ref=wfull.at[core],
@@ -105,9 +115,11 @@
     )
     swap.start()
 
-    chosen = jnp.concatenate([sub[s : s + 1, :] for s in range(ns)], axis=1)
+    for copy in small:
+        copy.wait()
     keep.wait()
     swap.wait()
+    chosen = jnp.concatenate([sub[s : s + 1, :] for s in range(ns)], axis=1)
     sides = []
     for iq in range(2):
         cols = []
@@ -126,12 +138,12 @@
         wst[s, 1] = lo
     flat = jnp.concatenate([jnp.concatenate(cols, axis=1) for cols in sides], axis=0)
     w_hi, w_lo = split(flat)
-    for ch in range(2):
+    for ch in range(4):
         r = lax.broadcasted_iota(jnp.int32, (rows, chans), 0)
         if c_loc % 8 == 0:
             chan = r + ch * rows
         else:
-            chan = (ch * half + r % half) * c_loc + r // half
+            chan = (ch * part + r % part) * c_loc + r // part
         pick = jnp.where(chan == chosen, 1.0, 0.0).astype(F32)
         pick_b = pick.astype(BF16)
         lhs[ch, 0:chans, :] = jnp.transpose(pick).astype(BF16)
@@ -140,26 +152,25 @@
 
     lanes = GB * pulses
     e_re = e_im = None
-    for q in range(2):
-        mine = me // half
-        ch = mine if q == 0 else 1 - mine
+    for q in (0, 1, 2, 3):
+        ch = partner(me // part, q, 4)
 
         def arrive(t, c):
             src = partner(me, t, n)
             piece(src, src, src).wait_recv()
             return c
 
-        lax.fori_loop(1 if q == 0 else half, half if q == 0 else n, arrive, 0)
+        lax.fori_loop(max(1, q * part), (q + 1) * part, arrive, 0)
         parts = []
         for iq in range(2):
             for g in range(GB):
                 j = (g * 2 + iq) * c_loc
                 if c_loc % 8 == 0:
-                    block = recv[pl.ds(ch * half, half), j : j + c_loc, :].reshape(rows, pulses)
+                    block = recv[pl.ds(ch * part, part), j : j + c_loc, :].reshape(rows, pulses)
                 else:
                     block = jnp.concatenate(
                         [
-                            recv[pl.ds(ch * half, half), j + c : j + c + 1, :].reshape(half, pulses)
+                            recv[pl.ds(ch * part, part), j + c : j + c + 1, :].reshape(part, pulses)
                             for c in range(c_loc)
                         ],
                         axis=0,
@@ -169,21 +180,23 @@
         z_hi, z_lo = split(z)
         l_hi = lhs[ch, chans : chans + 2 * beams, :]
         l_lo = lhs[ch, chans + 2 * beams : chans + 4 * beams, :]
-        part = dot(l_hi, z_hi) + (dot(l_hi, z_lo) + dot(l_lo, z_hi))
+        term = dot(l_hi, z_hi) + (dot(l_hi, z_lo) + dot(l_lo, z_hi))
         if q == 0:
-            sacc[...] = part
+            sacc[...] = term
+        elif q != 3:
+            sacc[...] = sacc[...] + term
         else:
-            full = sacc[...] + part
+            full = sacc[...] + term
             e_re = full[:beams, :lanes] + full[beams:, lanes:]
             e_im = full[:beams, lanes:] - full[beams:, :lanes]
             p_hi, p_lo = split(e_re * e_re + e_im * e_im)
             ones = jnp.ones((8, lanes), BF16)
-            esum = dot_t(ones, p_hi) + dot_t(ones, p_lo)
+            esum = (dot_t(ones, p_hi) + dot_t(ones, p_lo))[0:1]
             esend[...] = esum
             erecv[me] = esum
 
             def share(t, c):
-                d = partner(me, t, n)
+                d = partner(me, n - t, n)
                 report(d, me, d).start()
                 return c
 
@@ -246,7 +259,16 @@
 
     lax.fori_loop(1, n, close, 0)
     total = jnp.sum(erecv[...], axis=0)
-    en[...] = total[0:1, :] * (1.0 / (gates * pulses))
+    en[...] = total * (1.0 / (gates * pulses))
+
+
+def store(cov, filt, en, cov_out, filt_out, en_out, sem):
+    pairs = ((cov, cov_out), (filt, filt_out), (en, en_out))
+    copies = [pltpu.make_async_copy(a, b, sem.at[i]) for i, (a, b) in enumerate(pairs)]
+    for copy in copies:
+        copy.start()
+    for copy in copies:
+        copy.wait()
 
 
 def body(samples, beam_weights, subarrays, training):
@@ -266,30 +288,32 @@
     cov, filt, en = pl.pallas_call(
         functools.partial(kernel, dims),
         out_shape=(
-            jax.ShapeDtypeStruct((ns, s_n, 2 * s_n), F32),
-            jax.ShapeDtypeStruct((2, beams * GB, pulses), F32),
-            jax.ShapeDtypeStruct((1, beams), F32),
+            pltpu.VMEM((ns, s_n, 2 * s_n), F32),
+            pltpu.VMEM((2, beams * GB, pulses), F32),
+            pltpu.VMEM((1, beams), F32),
         ),
-        in_specs=[hbm, hbm, vmem, pl.BlockSpec(memory_space=pltpu.SMEM)],
+        in_specs=[hbm] * 4,
         out_specs=(vmem, vmem, vmem),
         scratch_shapes=[
+            pltpu.VMEM((ns, s_n), jnp.int32),
+            pltpu.SMEM((GB,), jnp.int32),
             pltpu.VMEM((2 * c_loc * gates, pulses), F32),
             pltpu.VMEM((n, 2 * GB * c_loc, pulses), F32),
             pltpu.VMEM((n, 2 * GB * c_loc, pulses), F32),
             pltpu.VMEM((2, ns, 2, s_n, k_half), F32),
-            pltpu.VMEM((2, chans + 4 * beams, chans // 2), BF16),
+            pltpu.VMEM((4, chans + 4 * beams, chans // 4), BF16),
             pltpu.VMEM((ns, 2, 2 * beams, s_n), BF16),
             pltpu.VMEM((ns, 2 * beams, 2 * s_n), F32),
             pltpu.VMEM((2 * beams, 2 * lanes), F32),
             pltpu.VMEM((2, chans, 2 * lanes), F32),
-            pltpu.VMEM((8, beams), F32),
-            pltpu.VMEM((n, 8, beams), F32),
+            pltpu.VMEM((1, beams), F32),
+            pltpu.VMEM((n, 1, beams), F32),
             dma((n,)),
             dma((n,)),
             dma((2,)),
             dma((n,)),
             dma((n,)),
-            dma((2,)),
+            dma((4,)),
         ],
         compiler_params=pltpu.CompilerParams(collective_id=0, has_side_effects=True),
     )(
@@ -298,6 +322,14 @@
         subarrays.reshape(ns, s_n),
         training,
     )
+    cov, filt, en = (pltpu.with_memory_space_constraint(v, pltpu.VMEM) for v in (cov, filt, en))
+    cov, filt, en = pl.pallas_call(
+        store,
+        out_shape=[jax.ShapeDtypeStruct(v.shape, F32) for v in (cov, filt, en)],
+        in_specs=[vmem] * 3,
+        out_specs=[hbm] * 3,
+        scratch_shapes=[dma((3,))],
+    )(cov, filt, en)
     return (
         cov.reshape(1, ns, s_n, 2 * s_n),
         filt.reshape(2, beams, GB, pulses),

time: 41.9 us -> 36.8 us (0.88)
  local copies, waits for them, and re-layouts: 2.94 us -> 0 us
  Pallas kernels: 38.1 us -> 36 us
    unnamed x7 -> x0, local copies, waits for them, and re-layouts: 2.94 us -> none
    pallas_call x1 -> x2, Pallas kernels: 38.1 us -> 36 us  [the longest x1 35.2 us: body(): pl.pallas_call(functools.partial(kernel, dims), out_shape=(pltpu.VMEM((ns...]
where the time goes in v2:
time: 36.8 us; the launch traced here: 36.6 us
  Pallas kernels  36 us (98%)
  between operations  0.64 us (2%)
    pallas_call x1, Pallas kernels, body(): pl.pallas_call(functools.partial(kernel, dims), out_shape=(pltpu.VMEM((ns...  35.2 us
    pallas_call x1, Pallas kernels, body(): pl.pallas_call(store, out_shape=[jax.ShapeDtypeStruct(v.shape, F32) for v...  0.82 us

profile of v2, /device:TPU:0, one launch (start us, length us, event | category | flops | bytes accessed | tf_op | source)
XLA Modules:
  0.0 36.6 jit_solution(2844402101704460924)
XLA Ops:
  0.6 35.2 %shard_map.67 = (f32[8,64,128]{2,1,0:T(8,128)S(1)}, f32[2,256,128]{2,1,0:T(8,128)S(1)}, f32[1,128]{1,0:T(1,128)S(1)}) custom-call(f32[2048,128]{1,0:T(8,128)} %bitcast.5, f32[2,8,2,64,64]{4,3,2,1,0:T(8,128)} %bw.1, s32[8,64]{1,0:T(8,128)} %bitcast.6, s32[2]{0:T(128)} %trn_in.1), custom_call_target="tpu_custom_call" | custom-call | tf_op jit(solution)/shard_map/pallas_call | solution.py:288
  35.8 0.8 %shard_map.68 = (f32[8,64,128]{2,1,0:T(8,128)}, f32[2,256,128]{2,1,0:T(8,128)}, f32[1,128]{1,0:T(1,128)}) custom-call(f32[8,64,128]{2,1,0:T(8,128)S(1)} %get-tuple-element.9.cov, f32[2,256,128]{2,1,0:T(8,128)S(1)} %get-tuple-element.10.filt, f32[1,128]{1,0:T(1,128)S(1)} %get-tuple-element.11.en), custom_call_target="tpu_custom_call" | custom-call | tf_op jit(solution)/shard_map/pallas_call | solution.py:326
